TPU v7x, 8 devices: a whole 2x2x1 slice. The times are simulated.
8 devices in a mesh: dp: 2 (over z, y), sp: 4 (over x, core).
Axes of the slice: x: 2, y: 2, z: 1, core: 2. Of those that a mesh axis runs over, the one named last changes fastest.
Arguments:
- signal: bfloat16 [65536, 768], P(('dp', 'sp')), parts along dimension 0
- w_first: bfloat16 [8, 256, 2, 128, 128], P(None, 'sp')
- w_second: bfloat16 [8, 256, 2, 128, 128], P(None, 'sp')
Outputs:
- output: bfloat16 [65536, 768], P(('dp', 'sp')), parts along dimension 0
There are 2 independent parts. A program takes and returns all parts, laid end to end along the dimension named above; an argument that names none is the same for every part.
All inputs are finite; a program needn't handle non-finite values.
Results may differ from a plain program's by a relative error of at most 0.02.
Values are sent between devices in bfloat16 or wider.
A program may use at most 1 GiB of HBM per device.

v0:
```python
import functools

import jax
import jax.numpy as jnp
from jax import lax
from jax.experimental import pallas as pl
from jax.experimental.pallas import tpu as pltpu
from jax.sharding import PartitionSpec as P


WIDTH = 256
LAST_PIECES = (32, 16, 16)

ERFC_P = (2.326819970068386e-2, -1.387039388740657e-1, 3.687424674597105e-1, -5.824733027278666e-1, 6.210004621745983e-1,
          -4.944515323274145e-1, 3.404879937665872e-1, -2.741127028184656e-1, 5.638259427386472e-1)
ERFC_R = (-1.047766399936249e1, 1.297719955372516e1, -7.495518717768503e0, 2.921019019210786e0, -1.015265279202700e0,
          4.218463358204948e-1, -2.820767439740514e-1, 5.641895067754075e-1)


def horner(coeffs, y):
    total = jnp.full_like(y, coeffs[0])
    for c in coeffs[1:]:
        total = total * y + c
    return total


def gelu(x):
    a = x * (-(0.5 ** 0.5))
    mag = jnp.abs(a)
    far = jnp.maximum(mag, 1.0)
    q = 1.0 / far
    y = q * q
    poly = jnp.where(far < 2.0, horner(ERFC_P, y), horner(ERFC_R, y))
    tail = jnp.exp(-far * far) * q * poly
    tail = jnp.where(a < 0.0, 2.0 - tail, tail)
    return 0.5 * x * jnp.where(mag < 1.0, 1.0 - lax.erf(a), tail)


def mix(w_own, w_cross, z_own, z_cross):
    weights = jnp.concatenate([w_own, w_cross], axis=1)
    blocks = jnp.concatenate([z_own, z_cross], axis=0)
    return jnp.dot(weights, blocks, preferred_element_type=jnp.float32)


def cross_kernel(blocks, *refs):
    own, partner, w, out = refs[0], refs[1], refs[2], refs[-1]
    size = w.shape[-1]
    for b in range(blocks):
        rows = pl.ds(b * size, size)
        out[rows, :] = mix(w[0, b, 0], w[0, b, 1], own[rows, :], partner[rows, :]).astype(out.dtype)


def cross_stage(own, partner, weights, stage, first, count, width, own_at, partner_at, out_shape, out_at, into=None, after=(), blocks=8):
    size = weights.shape[-1]
    any_space = pl.BlockSpec(memory_space=pl.ANY)

    def spec(at):
        row, col = at
        return pl.BlockSpec((blocks * size, width), lambda g: (row // blocks + g, col))

    operands = [own, partner, weights]
    in_specs = [
        spec(own_at),
        spec(partner_at),
        pl.BlockSpec((1, blocks, 2, size, size), lambda g: (stage, first // blocks + g, 0, 0, 0)),
    ]
    aliases = {}
    if into is not None:
        aliases = {len(operands): 0}
        operands.append(into)
    operands += after
    in_specs += [any_space] * (len(operands) - len(in_specs))
    rows = count * size
    return pl.pallas_call(
        functools.partial(cross_kernel, blocks),
        grid=(count // blocks,),
        out_shape=jax.ShapeDtypeStruct(out_shape, own.dtype),
        in_specs=in_specs,
        out_specs=spec(out_at),
        input_output_aliases=aliases,
        compiler_params=pltpu.CompilerParams(dimension_semantics=("arbitrary",)),
        cost_estimate=pl.CostEstimate(
            flops=4 * rows * size * width, bytes_accessed=6 * rows * width + 4 * rows * size, transcendentals=0),
        name="cross_stage",
    )(*operands)


def local_kernel(first_steps, own, partner, wf, ws, out, other):
    step = pl.program_id(0)
    local, size = wf.shape[1], wf.shape[-1]

    @pl.when(step == 0)
    def _():
        def body(b, carry):
            rows = pl.ds(pl.multiple_of(b * size, size), size)
            out[rows, :] = mix(wf[0, b, 0], wf[0, b, 1], own[rows, :], partner[rows, :]).astype(out.dtype)
            return carry

        lax.fori_loop(0, local, body, 0, unroll=8)

    def stage(w, src, dst, shift, act):
        def body(p, carry):
            i = lax.shift_left(lax.shift_right_logical(p, shift), shift + 1) + (p & (lax.shift_left(1, shift) - 1))
            j = i + lax.shift_left(1, shift)
            ri = pl.ds(pl.multiple_of(i * size, size), size)
            rj = pl.ds(pl.multiple_of(j * size, size), size)
            zi, zj = src[ri, :], src[rj, :]
            blocks = jnp.concatenate([zi, zj], axis=0)
            weights = jnp.concatenate([
                jnp.concatenate([w[0, i, 0], w[0, i, 1]], axis=1),
                jnp.concatenate([w[0, j, 1], w[0, j, 0]], axis=1),
            ], axis=0)
            mixed = jnp.dot(weights, blocks, preferred_element_type=jnp.float32)
            mixed = mixed.astype(dst.dtype)
            if act:
                mixed = gelu(mixed.astype(jnp.float32)).astype(dst.dtype)
            dst[ri, :] = mixed[:size]
            dst[rj, :] = mixed[size:]
            return carry

        lax.fori_loop(0, local // 2, body, 0, unroll=1 if act else 4)

    odd = (step % 2) == 1

    @pl.when(jnp.logical_and(jnp.logical_and(step >= 1, step < first_steps), odd))
    def _():
        stage(wf, out, other, first_steps - step, False)

    @pl.when(jnp.logical_and(jnp.logical_and(step >= 1, step < first_steps), jnp.logical_not(odd)))
    def _():
        stage(wf, other, out, first_steps - step, False)

    @pl.when(step == first_steps)
    def _():
        if first_steps % 2:
            stage(wf, out, other, 0, True)
        else:
            stage(wf, other, out, 0, True)

    @pl.when(jnp.logical_and(step > first_steps, odd))
    def _():
        stage(ws, out, other, step - first_steps - 1, False)

    @pl.when(jnp.logical_and(step > first_steps, jnp.logical_not(odd)))
    def _():
        stage(ws, other, out, step - first_steps - 1, False)


def local_stages(own, partner, w_first, w_second, skip):
    stages, local, _, size, _ = w_first.shape
    rows, width = own.shape
    first_steps = stages - skip
    steps = 1 + 2 * first_steps
    whole = pl.BlockSpec((rows, width), lambda t: (0, 0))
    w_block = (1, local, 2, size, size)
    flops = 4 * rows * size * width * steps
    return pl.pallas_call(
        functools.partial(local_kernel, first_steps),
        grid=(steps,),
        out_shape=jax.ShapeDtypeStruct((rows, width), own.dtype),
        in_specs=[
            whole,
            whole,
            pl.BlockSpec(w_block, lambda t: (jnp.minimum(t + skip - 1, stages - 1), 0, 0, 0, 0)),
            pl.BlockSpec(w_block, lambda t: (jnp.maximum(t - first_steps - 1, 0), 0, 0, 0, 0)),
        ],
        out_specs=whole,
        scratch_shapes=[pltpu.VMEM((rows, width), own.dtype)],
        compiler_params=pltpu.CompilerParams(dimension_semantics=("arbitrary",), vmem_limit_bytes=60 * 1024 * 1024),
        cost_estimate=pl.CostEstimate(flops=flops, bytes_accessed=6 * rows * width + 4 * rows * size * steps, transcendentals=0),
        name="local_stages",
    )(own, partner, w_first, w_second)


def solution(mesh):
    groups = mesh.shape["sp"]

    def swap(array, dev_step):
        return lax.ppermute(array, "sp", [(device, device ^ dev_step) for device in range(groups)])

    def device_program(signal, w_first, w_second):
        stages, local = w_first.shape[:2]
        rows, cols = signal.shape
        size = w_first.shape[-1]
        far = (2 ** (stages - 1)) // local
        near = far // 2
        width = WIDTH
        sent, source = [], signal
        for c in range(cols // width):
            chunk = source[:, c * width:(c + 1) * width]
            source, chunk = lax.optimization_barrier((source, chunk))
            sent.append(swap(chunk, far))
        late, done = [], ()
        for c, partner in enumerate(sent):
            act = cross_stage(signal, partner, w_first, 0, 0, local, width, (0, c), (0, 0), (rows, width), (0, 0), after=done)
            act = local_stages(act, swap(act, near), w_first, w_second, 2)
            partner = swap(act, near)
            pieces = LAST_PIECES if c == cols // width - 1 else (local,)
            first = 0
            for count in pieces:
                piece = cross_stage(act, partner, w_second, stages - 2, first, count, width, (first, 0), (first, 0),
                                    (count * size, width), (0, 0))
                late.append((c, first, count, piece, swap(piece, far)))
                first += count
            done = [piece]
        result = None
        for c, first, count, piece, partner in late:
            result = cross_stage(piece, partner, w_second, stages - 1, first, count, width, (0, 0), (0, 0), (rows, cols), (first, c),
                                 into=result, after=done)
        return result

    row_spec = P(("dp", "sp"), None)
    weight_spec = P(None, "sp", None, None, None)
    return jax.shard_map(device_program, mesh=mesh, in_specs=(row_spec, weight_spec, weight_spec), out_specs=row_spec, check_vma=False)
```

profile of v0, /device:TPU:0, one launch (start us, length us, event | category | flops | bytes accessed | tf_op | source)
XLA Modules:
  0.0 793.4 jit_solution(17237302841967868808)
XLA Ops:
  0.0 2.5 slice.9
  2.5 3.3 collective-permute-start.2
  5.8 90.7 %collective-permute-done.2.refs_1_ = bf16[8192,256]{1,0:T(8,128)(2,1)} collective-permute-done((bf16[8192,256]{1,0:T(8,128)(2,1)S(1)}, bf16[8192,256]{1,0:T(8,128)(2,1)}, u32[]{:S(2)}, u32[]{:S(2)}) %collective-permute-start.2) | collective-permute-done | bytes 4194336 | tf_op jit(solution)/shard_map/ppermute | solution.py:179
  96.5 9.3 %cross_stage.13.own = bf16[8192,256]{1,0:T(8,128)(2,1)} custom-call(bf16[8192,768]{1,0:T(8,128)(2,1)} %refs_0_.5, bf16[8192,256]{1,0:T(8,128)(2,1)} %collective-permute-done.2.refs_1_, bf16[8,64,2,128,128]{4,3,2,1,0:T(8,128)(2,1)} %wf.5), custom_call_target="tpu_custom_call" | custom-call | flops 1073741824 | bytes 16777216 | tf_op jit(solution)/shard_map/cross_stage/pallas_call | solution.py:74
  105.8 7.5 collective-permute-done.3.partner
  113.3 58.3 %local_stages.3.refs_0_ = bf16[8192,256]{1,0:T(8,128)(2,1)} custom-call(bf16[8192,256]{1,0:T(8,128)(2,1)} %cross_stage.13.own, bf16[8192,256]{1,0:T(8,128)(2,1)} %collective-permute-done.3.partner, bf16[8,64,2,128,128]{4,3,2,1,0:T(8,128)(2,1)} %wf.5, bf16[8,64,2,128,128]{4,3,2,1,0:T(8,128)(2,1)} %refs_2_.25), custom_call_target="tpu_custom_call" | custom-call | flops 13958643712 | bytes 67108864 | tf_op jit(solution)/shard_map/local_stages/pallas_call | solution.py:157
  171.7 4.5 slice.10
  179.1 9.3 %cross_stage.14.refs_3_.refs_0_ = bf16[8192,256]{1,0:T(8,128)(2,1)} custom-call(bf16[8192,256]{1,0:T(8,128)(2,1)} %local_stages.3.refs_0_, bf16[8192,256]{1,0:T(8,128)(2,1)} %collective-permute-done.4.refs_1_, bf16[8,64,2,128,128]{4,3,2,1,0:T(8,128)(2,1)} %refs_2_.25), custom_call_target="tpu_custom_call" | custom-call | flops 1073741824 | bytes 16777216 | tf_op jit(solution)/shard_map/cross_stage/pallas_call | solution.py:74
  188.4 81.0 %collective-permute-done.1.refs_1_ = bf16[8192,256]{1,0:T(8,128)(2,1)} collective-permute-done((bf16[8192,256]{1,0:T(8,128)(2,1)}, bf16[8192,256]{1,0:T(8,128)(2,1)}, u32[]{:S(2)}, u32[]{:S(2)}) %collective-permute-start.1) | collective-permute-done | bytes 4194336 | tf_op jit(solution)/shard_map/ppermute | solution.py:179
  269.4 9.3 %cross_stage.15.own = bf16[8192,256]{1,0:T(8,128)(2,1)} custom-call(bf16[8192,768]{1,0:T(8,128)(2,1)} %refs_0_.5, bf16[8192,256]{1,0:T(8,128)(2,1)} %collective-permute-done.1.refs_1_, bf16[8,64,2,128,128]{4,3,2,1,0:T(8,128)(2,1)} %wf.5, bf16[8192,256]{1,0:T(8,128)(2,1)} %cross_stage.14.refs_3_.refs_0_), custom_call_target="tpu_custom_call" | custom-call | flops 1073741824 | bytes 16777216 | tf_op jit(solution)/shard_map/cross_stage/pallas_call | solution.py:74
  278.7 7.5 collective-permute-done.5.partner
  286.2 58.3 %local_stages.4.refs_0_ = bf16[8192,256]{1,0:T(8,128)(2,1)} custom-call(bf16[8192,256]{1,0:T(8,128)(2,1)} %cross_stage.15.own, bf16[8192,256]{1,0:T(8,128)(2,1)} %collective-permute-done.5.partner, bf16[8,64,2,128,128]{4,3,2,1,0:T(8,128)(2,1)} %wf.5, bf16[8,64,2,128,128]{4,3,2,1,0:T(8,128)(2,1)} %refs_2_.25), custom_call_target="tpu_custom_call" | custom-call | flops 13958643712 | bytes 67108864 | tf_op jit(solution)/shard_map/local_stages/pallas_call | solution.py:157
  344.6 4.5 slice.11
  352.0 9.3 %cross_stage.16.refs_3_.refs_0_ = bf16[8192,256]{1,0:T(8,128)(2,1)} custom-call(bf16[8192,256]{1,0:T(8,128)(2,1)} %local_stages.4.refs_0_, bf16[8192,256]{1,0:T(8,128)(2,1)} %collective-permute-done.6.refs_1_, bf16[8,64,2,128,128]{4,3,2,1,0:T(8,128)(2,1)} %refs_2_.25), custom_call_target="tpu_custom_call" | custom-call | flops 1073741824 | bytes 16777216 | tf_op jit(solution)/shard_map/cross_stage/pallas_call | solution.py:74
  361.3 80.9 %collective-permute-done.refs_1_ = bf16[8192,256]{1,0:T(8,128)(2,1)} collective-permute-done((bf16[8192,256]{1,0:T(8,128)(2,1)}, bf16[8192,256]{1,0:T(8,128)(2,1)}, u32[]{:S(2)}, u32[]{:S(2)}) %collective-permute-start) | collective-permute-done | bytes 4194336 | tf_op jit(solution)/shard_map/ppermute | solution.py:179
  442.3 9.3 %cross_stage.17.own = bf16[8192,256]{1,0:T(8,128)(2,1)} custom-call(bf16[8192,768]{1,0:T(8,128)(2,1)} %refs_0_.5, bf16[8192,256]{1,0:T(8,128)(2,1)} %collective-permute-done.refs_1_, bf16[8,64,2,128,128]{4,3,2,1,0:T(8,128)(2,1)} %wf.5, bf16[8192,256]{1,0:T(8,128)(2,1)} %cross_stage.16.refs_3_.refs_0_), custom_call_target="tpu_custom_call" | custom-call | flops 1073741824 | bytes 16777216 | tf_op jit(solution)/shard_map/cross_stage/pallas_call | solution.py:74
  451.6 7.5 collective-permute-done.7.partner
  459.1 58.3 %local_stages.5.refs_0_ = bf16[8192,256]{1,0:T(8,128)(2,1)} custom-call(bf16[8192,256]{1,0:T(8,128)(2,1)} %cross_stage.17.own, bf16[8192,256]{1,0:T(8,128)(2,1)} %collective-permute-done.7.partner, bf16[8,64,2,128,128]{4,3,2,1,0:T(8,128)(2,1)} %wf.5, bf16[8,64,2,128,128]{4,3,2,1,0:T(8,128)(2,1)} %refs_2_.25), custom_call_target="tpu_custom_call" | custom-call | flops 13958643712 | bytes 67108864 | tf_op jit(solution)/shard_map/local_stages/pallas_call | solution.py:157
  519.5 5.3 collective-permute-done.8.refs_1_
  524.9 5.1 cross_stage.20.refs_0_
  531.7 2.9 cross_stage.19.refs_0_
  534.9 2.9 cross_stage.18.refs_3_.refs_4_.refs_0_
  539.6 71.6 %collective-permute-done.13.refs_1_ = bf16[8192,256]{1,0:T(8,128)(2,1)} collective-permute-done((bf16[8192,256]{1,0:T(8,128)(2,1)}, bf16[8192,256]{1,0:T(8,128)(2,1)}, u32[]{:S(2)}, u32[]{:S(2)}) %collective-permute-start.13) | collective-permute-done | bytes 4194336 | tf_op jit(solution)/shard_map/ppermute | solution.py:179
  611.3 9.3 %cross_stage.21.refs_3_ = bf16[8192,768]{1,0:T(8,128)(2,1)} custom-call(bf16[8192,256]{1,0:T(8,128)(2,1)} %cross_stage.14.refs_3_.refs_0_, bf16[8192,256]{1,0:T(8,128)(2,1)} %collective-permute-done.13.refs_1_, bf16[8,64,2,128,128]{4,3,2,1,0:T(8,128)(2,1)} %refs_2_.25, bf16[2048,256]{1,0:T(8,128)(2,1)} %cross_stage.18.refs_3_.refs_4_.refs_0_), custom_call_target="tpu_custom_call" | custom-call | flops 1073741824 | bytes 16777216 | tf_op jit(solution)/shard_map/cross_stage/pallas_call | solution.py:74
  620.5 80.6 %collective-permute-done.12.refs_1_ = bf16[8192,256]{1,0:T(8,128)(2,1)} collective-permute-done((bf16[8192,256]{1,0:T(8,128)(2,1)}, bf16[8192,256]{1,0:T(8,128)(2,1)}, u32[]{:S(2)}, u32[]{:S(2)}) %collective-permute-start.12) | collective-permute-done | bytes 4194336 | tf_op jit(solution)/shard_map/ppermute | solution.py:179
  701.1 9.3 %cross_stage.22.refs_3_ = bf16[8192,768]{1,0:T(8,128)(2,1)} custom-call(bf16[8192,256]{1,0:T(8,128)(2,1)} %cross_stage.16.refs_3_.refs_0_, bf16[8192,256]{1,0:T(8,128)(2,1)} %collective-permute-done.12.refs_1_, bf16[8,64,2,128,128]{4,3,2,1,0:T(8,128)(2,1)} %refs_2_.25, bf16[8192,768]{1,0:T(8,128)(2,1)} %cross_stage.21.refs_3_, ...), custom_call_target="tpu_custom_call", output_to_operand_aliasing={{}: (3, {})} | custom-call | flops 1073741824 | bytes 16777216 | tf_op jit(solution)/shard_map/cross_stage/pallas_call | solution.py:74
  710.4 35.6 %collective-permute-done.11.refs_1_ = bf16[4096,256]{1,0:T(8,128)(2,1)S(1)} collective-permute-done((bf16[4096,256]{1,0:T(8,128)(2,1)}, bf16[4096,256]{1,0:T(8,128)(2,1)S(1)}, u32[]{:S(2)}, u32[]{:S(2)}) %collective-permute-start.11) | collective-permute-done | bytes 2097184 | tf_op jit(solution)/shard_map/ppermute | solution.py:179
  747.3 5.1 cross_stage.23.refs_3_
  752.4 16.0 %collective-permute-done.10.refs_1_ = bf16[2048,256]{1,0:T(8,128)(2,1)S(1)} collective-permute-done((bf16[2048,256]{1,0:T(8,128)(2,1)}, bf16[2048,256]{1,0:T(8,128)(2,1)S(1)}, u32[]{:S(2)}, u32[]{:S(2)}) %collective-permute-start.10) | collective-permute-done | bytes 1048608 | tf_op jit(solution)/shard_map/ppermute | solution.py:179
  769.4 2.9 cross_stage.24.refs_3_
  772.4 18.0 %collective-permute-done.9.refs_1_ = bf16[2048,256]{1,0:T(8,128)(2,1)} collective-permute-done((bf16[2048,256]{1,0:T(8,128)(2,1)}, bf16[2048,256]{1,0:T(8,128)(2,1)}, u32[]{:S(2)}, u32[]{:S(2)}) %collective-permute-start.9) | collective-permute-done | bytes 1048608 | tf_op jit(solution)/shard_map/ppermute | solution.py:179
  790.4 2.9 cross_stage.25
  (19 shorter events, 14.3 us)
Async XLA Ops:
  2.5 94.0 %collective-permute-start.2 = (bf16[8192,256]{1,0:T(8,128)(2,1)S(1)}, bf16[8192,256]{1,0:T(8,128)(2,1)}, u32[]{:S(2)}, u32[]{:S(2)}) collective-permute-start(bf16[8192,256]{1,0:T(8,128)(2,1)S(1)} %slice.9), channel_id=1, source_target_pairs={{0,2},{1,3},{2,0},{3,1},{4,6},{5,7},{6,4},{7,5}} | collective-permute-start | bytes 12582920 | tf_op jit(solution)/shard_map/ppermute | solution.py:179
  105.8 7.5 collective-permute-start.3
  171.6 7.5 collective-permute-start.4
  176.2 93.2 %collective-permute-start.1 = (bf16[8192,256]{1,0:T(8,128)(2,1)}, bf16[8192,256]{1,0:T(8,128)(2,1)}, u32[]{:S(2)}, u32[]{:S(2)}) collective-permute-start(bf16[8192,256]{1,0:T(8,128)(2,1)} %slice.10), channel_id=1, source_target_pairs={{0,2},{1,3},{2,0},{3,1},{4,6},{5,7},{6,4},{7,5}} | collective-permute-start | bytes 12582920 | tf_op jit(solution)/shard_map/ppermute | solution.py:179
  278.7 7.5 collective-permute-start.5
  344.5 7.5 collective-permute-start.6
  349.1 93.2 %collective-permute-start = (bf16[8192,256]{1,0:T(8,128)(2,1)}, bf16[8192,256]{1,0:T(8,128)(2,1)}, u32[]{:S(2)}, u32[]{:S(2)}) collective-permute-start(bf16[8192,256]{1,0:T(8,128)(2,1)} %slice.11), channel_id=1, source_target_pairs={{0,2},{1,3},{2,0},{3,1},{4,6},{5,7},{6,4},{7,5}} | collective-permute-start | bytes 12582920 | tf_op jit(solution)/shard_map/ppermute | solution.py:179
  451.6 7.5 collective-permute-start.7
  517.4 7.5 collective-permute-start.8
  517.5 93.8 %collective-permute-start.13 = (bf16[8192,256]{1,0:T(8,128)(2,1)}, bf16[8192,256]{1,0:T(8,128)(2,1)}, u32[]{:S(2)}, u32[]{:S(2)}) collective-permute-start(bf16[8192,256]{1,0:T(8,128)(2,1)} %cross_stage.14.refs_3_.refs_0_), channel_id=1, source_target_pairs={{0,2},{1,3},{2,0},{3,1},{4,6},{5,7},{6,4},{7,5}} | collective-permute-start | bytes 12582920 | tf_op jit(solution)/shard_map/ppermute | solution.py:179
  519.2 181.9 %collective-permute-start.12 = (bf16[8192,256]{1,0:T(8,128)(2,1)}, bf16[8192,256]{1,0:T(8,128)(2,1)}, u32[]{:S(2)}, u32[]{:S(2)}) collective-permute-start(bf16[8192,256]{1,0:T(8,128)(2,1)} %cross_stage.16.refs_3_.refs_0_), channel_id=1, source_target_pairs={{0,2},{1,3},{2,0},{3,1},{4,6},{5,7},{6,4},{7,5}} | collective-permute-start | bytes 12582920 | tf_op jit(solution)/shard_map/ppermute | solution.py:179
  530.0 216.0 %collective-permute-start.11 = (bf16[4096,256]{1,0:T(8,128)(2,1)}, bf16[4096,256]{1,0:T(8,128)(2,1)S(1)}, u32[]{:S(2)}, u32[]{:S(2)}) collective-permute-start(bf16[4096,256]{1,0:T(8,128)(2,1)} %cross_stage.20.refs_0_), channel_id=1, source_target_pairs={{0,2},{1,3},{2,0},{3,1},{4,6},{5,7},{6,4},{7,5}} | collective-permute-start | bytes 6291464 | tf_op jit(solution)/shard_map/ppermute | solution.py:179
  534.6 233.8 %collective-permute-start.10 = (bf16[2048,256]{1,0:T(8,128)(2,1)}, bf16[2048,256]{1,0:T(8,128)(2,1)S(1)}, u32[]{:S(2)}, u32[]{:S(2)}) collective-permute-start(bf16[2048,256]{1,0:T(8,128)(2,1)} %cross_stage.19.refs_0_), channel_id=1, source_target_pairs={{0,2},{1,3},{2,0},{3,1},{4,6},{5,7},{6,4},{7,5}} | collective-permute-start | bytes 3145736 | tf_op jit(solution)/shard_map/ppermute | solution.py:179
  537.9 252.6 %collective-permute-start.9 = (bf16[2048,256]{1,0:T(8,128)(2,1)}, bf16[2048,256]{1,0:T(8,128)(2,1)}, u32[]{:S(2)}, u32[]{:S(2)}) collective-permute-start(bf16[2048,256]{1,0:T(8,128)(2,1)} %cross_stage.18.refs_3_.refs_4_.refs_0_), channel_id=1, source_target_pairs={{0,2},{1,3},{2,0},{3,1},{4,6},{5,7},{6,4},{7,5}} | collective-permute-start | bytes 3145736 | tf_op jit(solution)/shard_map/ppermute | solution.py:179
  746.0 1.3 copy-start
  768.4 1.0 copy-start.1
where the time goes:
time: 795 us; the launch traced here: 793 us
  waiting for transfers between devices  505 us (64%)
  Pallas kernels  262 us (33%)
  local copies, waits for them, and re-layouts  13.7 us (2%)
  starting transfers between devices  13 us (2%)
    ppermute x14, waiting for transfers between devices, swap(): lax.ppermute(array, 'sp', [(device, device ^ dev_step) for device in rang...  505 us
    pallas_call x3, Pallas kernels, local_stages(): pl.pallas_call(functools.partial(local_kernel, first_steps), grid=(steps,...  175 us
    pallas_call x13, Pallas kernels, cross_stage(): pl.pallas_call(functools.partial(cross_kernel, blocks), grid=(count // bl...  87.1 us
  transfers between devices with their start and end apart: 14, of which 14 were waited for; matrix products, arithmetic and copies ran while one was open for 1% of the time, Pallas kernels for 7%

commit v1 on v0

--- a/solution.py
+++ b/solution.py
@@ -9,7 +9,8 @@
 
 
 WIDTH = 256
-LAST_PIECES = (32, 16, 16)
+LAST_PIECES = (32, 16, 8, 4, 4)
+FIRST_PIECES = (8, 56)
 
 ERFC_P = (2.326819970068386e-2, -1.387039388740657e-1, 3.687424674597105e-1, -5.824733027278666e-1, 6.210004621745983e-1,
           -4.944515323274145e-1, 3.404879937665872e-1, -2.741127028184656e-1, 5.638259427386472e-1)
@@ -50,8 +51,8 @@
         out[rows, :] = mix(w[0, b, 0], w[0, b, 1], own[rows, :], partner[rows, :]).astype(out.dtype)
 
 
-def cross_stage(own, partner, weights, stage, first, count, width, own_at, partner_at, out_shape, out_at, into=None, after=(), blocks=8):
-    size = weights.shape[-1]
+def cross_stage(own, partner, weights, stage, first, count, width, own_at, partner_at, out_shape, out_at, into=None, after=()):
+    size, blocks = weights.shape[-1], min(count, 8)
     any_space = pl.BlockSpec(memory_space=pl.ANY)
 
     def spec(at):
@@ -187,12 +188,20 @@
         width = WIDTH
         sent, source = [], signal
         for c in range(cols // width):
-            chunk = source[:, c * width:(c + 1) * width]
-            source, chunk = lax.optimization_barrier((source, chunk))
-            sent.append(swap(chunk, far))
+            pieces = FIRST_PIECES if c == 0 else (local,)
+            first, parts = 0, []
+            for count in pieces:
+                piece = source[first * size:(first + count) * size, c * width:(c + 1) * width]
+                source, piece = lax.optimization_barrier((source, piece))
+                parts.append((first, count, swap(piece, far)))
+                first += count
+            sent.append(parts)
         late, done = [], ()
-        for c, partner in enumerate(sent):
-            act = cross_stage(signal, partner, w_first, 0, 0, local, width, (0, c), (0, 0), (rows, width), (0, 0), after=done)
+        for c, parts in enumerate(sent):
+            act = None
+            for first, count, partner in parts:
+                act = cross_stage(signal, partner, w_first, 0, first, count, width, (first, c), (0, 0), (rows, width), (first, 0),
+                                  into=act, after=done)
             act = local_stages(act, swap(act, near), w_first, w_second, 2)
             partner = swap(act, near)
             pieces = LAST_PIECES if c == cols // width - 1 else (local,)

time: 795 us -> 800 us (level)
  waiting for transfers between devices: 505 us -> 493 us
  Pallas kernels: 262 us -> 271 us
    ppermute x14 -> x17, waiting for transfers between devices: 505 us -> 493 us  [swap(): lax.ppermute(array, 'sp', [(device, device ^ dev_step) for device in rang...]
    pallas_call x13 -> x18, Pallas kernels: 87.1 us -> 96.3 us  [cross_stage(): pl.pallas_call(functools.partial(cross_kernel, blocks), grid=(count // bl...]
    ppermute x14 -> x17, starting transfers between devices: 13 us -> 16.5 us  [swap(): lax.ppermute(array, 'sp', [(device, device ^ dev_step) for device in rang...]
  transfers between devices with their start and end apart: 14 -> 17, of which waited for: 14 -> 16; matrix products, arithmetic and copies ran while one was open for 1% -> 1% of each run, Pallas kernels for 7% -> 8%
where the time goes in v1:
time: 800 us; the launch traced here: 798 us
  waiting for transfers between devices  493 us (62%)
  Pallas kernels  271 us (34%)
  local copies, waits for them, and re-layouts  17.2 us (2%)
  starting transfers between devices  16.5 us (2%)
    ppermute x17, waiting for transfers between devices, swap(): lax.ppermute(array, 'sp', [(device, device ^ dev_step) for device in rang...  493 us
    pallas_call x3, Pallas kernels, local_stages(): pl.pallas_call(functools.partial(local_kernel, first_steps), grid=(steps,...  175 us
    pallas_call x18, Pallas kernels, cross_stage(): pl.pallas_call(functools.partial(cross_kernel, blocks), grid=(count // bl...  96.3 us
    ppermute x17, starting transfers between devices, swap(): lax.ppermute(array, 'sp', [(device, device ^ dev_step) for device in rang...  16.5 us
  transfers between devices with their start and end apart: 17, of which 16 were waited for; matrix products, arithmetic and copies ran while one was open for 1% of the time, Pallas kernels for 8%

profile of v1, /device:TPU:0, one launch (start us, length us, event | category | flops | bytes accessed | tf_op | source)
XLA Modules:
  0.0 798.0 jit_solution(14706006871860646748)
XLA Ops:
  1.1 4.1 slice.13
  5.1 3.3 collective-permute-start.2
  8.5 90.8 %collective-permute-done.3.refs_1_ = bf16[1024,256]{1,0:T(8,128)(2,1)S(1)} collective-permute-done((bf16[1024,256]{1,0:T(8,128)(2,1)S(1)}, bf16[1024,256]{1,0:T(8,128)(2,1)S(1)}, u32[]{:S(2)}, u32[]{:S(2)}) %collective-permute-start.3) | collective-permute-done | bytes 524320 | tf_op jit(solution)/shard_map/ppermute | solution.py:180
  102.5 8.8 %cross_stage.19.own = bf16[8192,256]{1,0:T(8,128)(2,1)} custom-call(bf16[8192,768]{1,0:T(8,128)(2,1)} %refs_0_.7, bf16[7168,256]{1,0:T(8,128)(2,1)} %collective-permute-done.2.refs_1_, bf16[8,64,2,128,128]{4,3,2,1,0:T(8,128)(2,1)} %wf.5, bf16[8192,256]{1,0:T(8,128)(2,1)} %cross_stage.18.refs_3_), custom_call_target="tpu_custom_call", output_to_operand_aliasing={{}: (3, {})} | custom-call | flops 939524096 | bytes 14680064 | tf_op jit(solution)/shard_map/cross_stage/pallas_call | solution.py:75
  111.3 7.5 collective-permute-done.4.partner
  118.8 58.3 %local_stages.3.refs_0_ = bf16[8192,256]{1,0:T(8,128)(2,1)} custom-call(bf16[8192,256]{1,0:T(8,128)(2,1)} %cross_stage.19.own, bf16[8192,256]{1,0:T(8,128)(2,1)} %collective-permute-done.4.partner, bf16[8,64,2,128,128]{4,3,2,1,0:T(8,128)(2,1)} %wf.5, bf16[8,64,2,128,128]{4,3,2,1,0:T(8,128)(2,1)} %refs_2_.35), custom_call_target="tpu_custom_call" | custom-call | flops 13958643712 | bytes 67108864 | tf_op jit(solution)/shard_map/local_stages/pallas_call | solution.py:158
  177.3 4.5 slice.14
  184.6 9.3 %cross_stage.20.refs_3_.refs_0_ = bf16[8192,256]{1,0:T(8,128)(2,1)} custom-call(bf16[8192,256]{1,0:T(8,128)(2,1)} %local_stages.3.refs_0_, bf16[8192,256]{1,0:T(8,128)(2,1)} %collective-permute-done.5.refs_1_, bf16[8,64,2,128,128]{4,3,2,1,0:T(8,128)(2,1)} %refs_2_.35), custom_call_target="tpu_custom_call" | custom-call | flops 1073741824 | bytes 16777216 | tf_op jit(solution)/shard_map/cross_stage/pallas_call | solution.py:75
  193.9 81.0 %collective-permute-done.1.refs_1_ = bf16[8192,256]{1,0:T(8,128)(2,1)} collective-permute-done((bf16[8192,256]{1,0:T(8,128)(2,1)}, bf16[8192,256]{1,0:T(8,128)(2,1)}, u32[]{:S(2)}, u32[]{:S(2)}) %collective-permute-start.1) | collective-permute-done | bytes 4194336 | tf_op jit(solution)/shard_map/ppermute | solution.py:180
  274.9 9.3 %cross_stage.21.own = bf16[8192,256]{1,0:T(8,128)(2,1)} custom-call(bf16[8192,768]{1,0:T(8,128)(2,1)} %refs_0_.7, bf16[8192,256]{1,0:T(8,128)(2,1)} %collective-permute-done.1.refs_1_, bf16[8,64,2,128,128]{4,3,2,1,0:T(8,128)(2,1)} %wf.5, bf16[8192,256]{1,0:T(8,128)(2,1)} %cross_stage.20.refs_3_.refs_0_), custom_call_target="tpu_custom_call" | custom-call | flops 1073741824 | bytes 16777216 | tf_op jit(solution)/shard_map/cross_stage/pallas_call | solution.py:75
  284.2 7.5 collective-permute-done.6.partner
  291.7 58.3 %local_stages.4.refs_0_ = bf16[8192,256]{1,0:T(8,128)(2,1)} custom-call(bf16[8192,256]{1,0:T(8,128)(2,1)} %cross_stage.21.own, bf16[8192,256]{1,0:T(8,128)(2,1)} %collective-permute-done.6.partner, bf16[8,64,2,128,128]{4,3,2,1,0:T(8,128)(2,1)} %wf.5, bf16[8,64,2,128,128]{4,3,2,1,0:T(8,128)(2,1)} %refs_2_.35), custom_call_target="tpu_custom_call" | custom-call | flops 13958643712 | bytes 67108864 | tf_op jit(solution)/shard_map/local_stages/pallas_call | solution.py:158
  350.2 4.5 slice.15
  357.5 9.3 %cross_stage.22.refs_3_.refs_0_ = bf16[8192,256]{1,0:T(8,128)(2,1)} custom-call(bf16[8192,256]{1,0:T(8,128)(2,1)} %local_stages.4.refs_0_, bf16[8192,256]{1,0:T(8,128)(2,1)} %collective-permute-done.7.refs_1_, bf16[8,64,2,128,128]{4,3,2,1,0:T(8,128)(2,1)} %refs_2_.35), custom_call_target="tpu_custom_call" | custom-call | flops 1073741824 | bytes 16777216 | tf_op jit(solution)/shard_map/cross_stage/pallas_call | solution.py:75
  366.9 80.9 %collective-permute-done.refs_1_ = bf16[8192,256]{1,0:T(8,128)(2,1)} collective-permute-done((bf16[8192,256]{1,0:T(8,128)(2,1)}, bf16[8192,256]{1,0:T(8,128)(2,1)}, u32[]{:S(2)}, u32[]{:S(2)}) %collective-permute-start) | collective-permute-done | bytes 4194336 | tf_op jit(solution)/shard_map/ppermute | solution.py:180
  447.8 9.3 %cross_stage.23.own = bf16[8192,256]{1,0:T(8,128)(2,1)} custom-call(bf16[8192,768]{1,0:T(8,128)(2,1)} %refs_0_.7, bf16[8192,256]{1,0:T(8,128)(2,1)} %collective-permute-done.refs_1_, bf16[8,64,2,128,128]{4,3,2,1,0:T(8,128)(2,1)} %wf.5, bf16[8192,256]{1,0:T(8,128)(2,1)} %cross_stage.22.refs_3_.refs_0_), custom_call_target="tpu_custom_call" | custom-call | flops 1073741824 | bytes 16777216 | tf_op jit(solution)/shard_map/cross_stage/pallas_call | solution.py:75
  457.1 7.5 collective-permute-done.8.partner
  464.6 58.3 %local_stages.5.refs_0_ = bf16[8192,256]{1,0:T(8,128)(2,1)} custom-call(bf16[8192,256]{1,0:T(8,128)(2,1)} %cross_stage.23.own, bf16[8192,256]{1,0:T(8,128)(2,1)} %collective-permute-done.8.partner, bf16[8,64,2,128,128]{4,3,2,1,0:T(8,128)(2,1)} %wf.5, bf16[8,64,2,128,128]{4,3,2,1,0:T(8,128)(2,1)} %refs_2_.35), custom_call_target="tpu_custom_call" | custom-call | flops 13958643712 | bytes 67108864 | tf_op jit(solution)/shard_map/local_stages/pallas_call | solution.py:158
  525.1 5.3 collective-permute-done.9.refs_1_
  530.4 5.1 cross_stage.28.refs_0_
  537.3 2.9 cross_stage.27.refs_0_
  548.9 67.9 %collective-permute-done.16.refs_1_ = bf16[8192,256]{1,0:T(8,128)(2,1)} collective-permute-done((bf16[8192,256]{1,0:T(8,128)(2,1)}, bf16[8192,256]{1,0:T(8,128)(2,1)}, u32[]{:S(2)}, u32[]{:S(2)}) %collective-permute-start.16) | collective-permute-done | bytes 4194336 | tf_op jit(solution)/shard_map/ppermute | solution.py:180
  618.6 88.1 %collective-permute-done.15.refs_1_ = bf16[8192,256]{1,0:T(8,128)(2,1)} collective-permute-done((bf16[8192,256]{1,0:T(8,128)(2,1)}, bf16[8192,256]{1,0:T(8,128)(2,1)}, u32[]{:S(2)}, u32[]{:S(2)}) %collective-permute-start.15) | collective-permute-done | bytes 4194336 | tf_op jit(solution)/shard_map/ppermute | solution.py:180
  708.4 9.3 %cross_stage.29.refs_3_ = bf16[8192,768]{1,0:T(8,128)(2,1)} custom-call(bf16[8192,256]{1,0:T(8,128)(2,1)} %cross_stage.20.refs_3_.refs_0_, bf16[8192,256]{1,0:T(8,128)(2,1)} %collective-permute-done.16.refs_1_, bf16[8,64,2,128,128]{4,3,2,1,0:T(8,128)(2,1)} %refs_2_.35, bf16[512,256]{1,0:T(8,128)(2,1)} %cross_stage.24.refs_3_.refs_4_.refs_0_), custom_call_target="tpu_custom_call" | custom-call | flops 1073741824 | bytes 16777216 | tf_op jit(solution)/shard_map/cross_stage/pallas_call | solution.py:75
  717.7 9.3 %cross_stage.30.refs_3_ = bf16[8192,768]{1,0:T(8,128)(2,1)} custom-call(bf16[8192,256]{1,0:T(8,128)(2,1)} %cross_stage.22.refs_3_.refs_0_, bf16[8192,256]{1,0:T(8,128)(2,1)} %collective-permute-done.15.refs_1_, bf16[8,64,2,128,128]{4,3,2,1,0:T(8,128)(2,1)} %refs_2_.35, bf16[8192,768]{1,0:T(8,128)(2,1)} %cross_stage.29.refs_3_, ...), custom_call_target="tpu_custom_call", output_to_operand_aliasing={{}: (3, {})} | custom-call | flops 1073741824 | bytes 16777216 | tf_op jit(solution)/shard_map/cross_stage/pallas_call | solution.py:75
  727.0 24.5 %collective-permute-done.14.refs_1_ = bf16[4096,256]{1,0:T(8,128)(2,1)S(1)} collective-permute-done((bf16[4096,256]{1,0:T(8,128)(2,1)}, bf16[4096,256]{1,0:T(8,128)(2,1)S(1)}, u32[]{:S(2)}, u32[]{:S(2)}) %collective-permute-start.14) | collective-permute-done | bytes 2097184 | tf_op jit(solution)/shard_map/ppermute | solution.py:180
  752.9 5.1 cross_stage.31.refs_3_
  758.0 16.0 %collective-permute-done.13.refs_1_ = bf16[2048,256]{1,0:T(8,128)(2,1)S(1)} collective-permute-done((bf16[2048,256]{1,0:T(8,128)(2,1)}, bf16[2048,256]{1,0:T(8,128)(2,1)S(1)}, u32[]{:S(2)}, u32[]{:S(2)}) %collective-permute-start.13) | collective-permute-done | bytes 1048608 | tf_op jit(solution)/shard_map/ppermute | solution.py:180
  775.0 2.9 cross_stage.32.refs_3_
  777.9 7.4 collective-permute-done.12.refs_1_
  787.8 3.2 collective-permute-done.11.refs_1_
  793.0 3.0 collective-permute-done.10.refs_1_
  (35 shorter events, 35.4 us)
Async XLA Ops:
  5.1 97.4 %collective-permute-start.2 = (bf16[7168,256]{1,0:T(8,128)(2,1)}, bf16[7168,256]{1,0:T(8,128)(2,1)}, u32[]{:S(2)}, u32[]{:S(2)}) collective-permute-start(bf16[7168,256]{1,0:T(8,128)(2,1)} %slice.13), channel_id=1, source_target_pairs={{0,2},{1,3},{2,0},{3,1},{4,6},{5,7},{6,4},{7,5}} | collective-permute-start | bytes 11010056 | tf_op jit(solution)/shard_map/ppermute | solution.py:180
  8.4 90.8 %collective-permute-start.3 = (bf16[1024,256]{1,0:T(8,128)(2,1)S(1)}, bf16[1024,256]{1,0:T(8,128)(2,1)S(1)}, u32[]{:S(2)}, u32[]{:S(2)}) collective-permute-start(bf16[1024,256]{1,0:T(8,128)(2,1)S(1)} %slice.12), channel_id=1, source_target_pairs={{0,2},{1,3},{2,0},{3,1},{4,6},{5,7},{6,4},{7,5}} | collective-permute-start | bytes 1572872 | tf_op jit(solution)/shard_map/ppermute | solution.py:180
  99.2 0.8 copy-start.3
  111.3 7.5 collective-permute-start.4
  177.1 7.5 collective-permute-start.5
  181.7 93.2 %collective-permute-start.1 = (bf16[8192,256]{1,0:T(8,128)(2,1)}, bf16[8192,256]{1,0:T(8,128)(2,1)}, u32[]{:S(2)}, u32[]{:S(2)}) collective-permute-start(bf16[8192,256]{1,0:T(8,128)(2,1)} %slice.14), channel_id=1, source_target_pairs={{0,2},{1,3},{2,0},{3,1},{4,6},{5,7},{6,4},{7,5}} | collective-permute-start | bytes 12582920 | tf_op jit(solution)/shard_map/ppermute | solution.py:180
  284.2 7.5 collective-permute-start.6
  350.0 7.5 collective-permute-start.7
  354.6 93.2 %collective-permute-start = (bf16[8192,256]{1,0:T(8,128)(2,1)}, bf16[8192,256]{1,0:T(8,128)(2,1)}, u32[]{:S(2)}, u32[]{:S(2)}) collective-permute-start(bf16[8192,256]{1,0:T(8,128)(2,1)} %slice.15), channel_id=1, source_target_pairs={{0,2},{1,3},{2,0},{3,1},{4,6},{5,7},{6,4},{7,5}} | collective-permute-start | bytes 12582920 | tf_op jit(solution)/shard_map/ppermute | solution.py:180
  457.1 7.5 collective-permute-start.8
  522.9 7.5 collective-permute-start.9
  523.1 93.8 %collective-permute-start.16 = (bf16[8192,256]{1,0:T(8,128)(2,1)}, bf16[8192,256]{1,0:T(8,128)(2,1)}, u32[]{:S(2)}, u32[]{:S(2)}) collective-permute-start(bf16[8192,256]{1,0:T(8,128)(2,1)} %cross_stage.20.refs_3_.refs_0_), channel_id=1, source_target_pairs={{0,2},{1,3},{2,0},{3,1},{4,6},{5,7},{6,4},{7,5}} | collective-permute-start | bytes 12582920 | tf_op jit(solution)/shard_map/ppermute | solution.py:180
  524.8 181.9 %collective-permute-start.15 = (bf16[8192,256]{1,0:T(8,128)(2,1)}, bf16[8192,256]{1,0:T(8,128)(2,1)}, u32[]{:S(2)}, u32[]{:S(2)}) collective-permute-start(bf16[8192,256]{1,0:T(8,128)(2,1)} %cross_stage.22.refs_3_.refs_0_), channel_id=1, source_target_pairs={{0,2},{1,3},{2,0},{3,1},{4,6},{5,7},{6,4},{7,5}} | collective-permute-start | bytes 12582920 | tf_op jit(solution)/shard_map/ppermute | solution.py:180
  535.5 216.0 %collective-permute-start.14 = (bf16[4096,256]{1,0:T(8,128)(2,1)}, bf16[4096,256]{1,0:T(8,128)(2,1)S(1)}, u32[]{:S(2)}, u32[]{:S(2)}) collective-permute-start(bf16[4096,256]{1,0:T(8,128)(2,1)} %cross_stage.28.refs_0_), channel_id=1, source_target_pairs={{0,2},{1,3},{2,0},{3,1},{4,6},{5,7},{6,4},{7,5}} | collective-permute-start | bytes 6291464 | tf_op jit(solution)/shard_map/ppermute | solution.py:180
  540.2 233.8 %collective-permute-start.13 = (bf16[2048,256]{1,0:T(8,128)(2,1)}, bf16[2048,256]{1,0:T(8,128)(2,1)S(1)}, u32[]{:S(2)}, u32[]{:S(2)}) collective-permute-start(bf16[2048,256]{1,0:T(8,128)(2,1)} %cross_stage.27.refs_0_), channel_id=1, source_target_pairs={{0,2},{1,3},{2,0},{3,1},{4,6},{5,7},{6,4},{7,5}} | collective-permute-start | bytes 3145736 | tf_op jit(solution)/shard_map/ppermute | solution.py:180
  543.0 242.4 %collective-permute-start.12 = (bf16[1024,256]{1,0:T(8,128)(2,1)}, bf16[1024,256]{1,0:T(8,128)(2,1)}, u32[]{:S(2)}, u32[]{:S(2)}) collective-permute-start(bf16[1024,256]{1,0:T(8,128)(2,1)} %cross_stage.26.refs_0_), channel_id=1, source_target_pairs={{0,2},{1,3},{2,0},{3,1},{4,6},{5,7},{6,4},{7,5}} | collective-permute-start | bytes 1572872 | tf_op jit(solution)/shard_map/ppermute | solution.py:180
  546.8 159.9 %copy-start = (bf16[512,256]{1,0:T(8,128)(2,1)S(1)}, bf16[512,256]{1,0:T(8,128)(2,1)}, u32[]{:S(2)}) copy-start(bf16[512,256]{1,0:T(8,128)(2,1)} %cross_stage.24.refs_3_.refs_4_.refs_0_) | copy-start | bytes 786436
  616.8 174.1 %collective-permute-start.11 = (bf16[512,256]{1,0:T(8,128)(2,1)}, bf16[512,256]{1,0:T(8,128)(2,1)}, u32[]{:S(2)}, u32[]{:S(2)}) collective-permute-start(bf16[512,256]{1,0:T(8,128)(2,1)} %cross_stage.25.refs_0_), channel_id=1, source_target_pairs={{0,2},{1,3},{2,0},{3,1},{4,6},{5,7},{6,4},{7,5}} | collective-permute-start | bytes 786440 | tf_op jit(solution)/shard_map/ppermute | solution.py:180
  706.7 89.3 %collective-permute-start.10 = (bf16[512,256]{1,0:T(8,128)(2,1)S(1)}, bf16[512,256]{1,0:T(8,128)(2,1)}, u32[]{:S(2)}, u32[]{:S(2)}) collective-permute-start(bf16[512,256]{1,0:T(8,128)(2,1)S(1)} %copy-done), channel_id=1, source_target_pairs={{0,2},{1,3},{2,0},{3,1},{4,6},{5,7},{6,4},{7,5}} | collective-permute-start | bytes 786440 | tf_op jit(solution)/shard_map/ppermute | solution.py:180
  751.5 1.3 copy-start.1
  774.0 1.0 copy-start.2
